TPU v7x, 64 devices: a 2x2x8 block of a 4x4x8 slice. The times are simulated.
64 devices in a mesh: dp: 4 (over x, y), sp: 16 (over z, core).
Axes of the slice: x: 2, y: 2, z: 8, core: 2. Of those that a mesh axis runs over, the one named last changes fastest.
The devices are a block of a 4x4x8 slice.
Arguments:
- q: bfloat16 [128, 32, 64], P('dp'), parts along dimension 0
- k: bfloat16 [128, 8192, 8, 64], P('dp', 'sp'), parts along dimension 0
- v: bfloat16 [128, 8192, 8, 64], P('dp', 'sp'), parts along dimension 0
Outputs:
- q: bfloat16 [128, 32, 64], P('dp'), parts along dimension 0
There are 4 independent parts. A program takes and returns all parts, laid end to end along the dimension named above; each array names one.
All inputs are finite; a program needn't handle non-finite values.
Results may differ from a plain program's by a relative error of at most 0.012.
Values are sent between devices in bfloat16 or wider.
A program may use at most 768 MiB of HBM per device.

v0:
```python
import jax
import jax.numpy as jnp
from jax import lax
from jax.sharding import PartitionSpec as P


def einsum(form, a, b):
    return jnp.einsum(form, a.astype(jnp.float32), b.astype(jnp.float32))


def part_of(q, k, v):
    grouped = q.reshape(q.shape[0], k.shape[2], -1, q.shape[2])
    scores = einsum("bgsd,bugd->bgsu", grouped, k) * q.shape[2] ** -0.5
    high = jnp.max(scores, -1, keepdims=True)
    weights = jnp.exp(scores - high)
    seen = einsum("bgsu,bugd->bgsd", weights.astype(jnp.bfloat16), v)
    return jnp.concatenate([seen, jnp.sum(weights, -1, keepdims=True), high], -1)


def together(parts):
    seen, total, high = parts[..., :-2], parts[..., -2:-1], parts[..., -1:]
    scale = jnp.exp(high - jnp.max(high, 0))
    return (jnp.sum(seen * scale, 0) / jnp.sum(total * scale, 0)).astype(jnp.bfloat16)


def solution(mesh):
    def step(q, k, v):
        return together(lax.all_gather(part_of(q, k, v), "sp")).reshape(q.shape)

    return jax.shard_map(
        step,
        mesh=mesh,
        in_specs=(P("dp", None, None), P("dp", "sp", None, None), P("dp", "sp", None, None)),
        out_specs=P("dp", None, None),
        check_vma=False,
    )
```

profile of v0, /device:TPU:21, one launch (start us, length us, event | category | flops | bytes accessed | tf_op | source)
XLA Modules:
  0.0 125.9 jit_solution(4425964083765211086)
XLA Ops:
  6.5 0.0 copy-start
  6.6 0.0 all-gather.3.cloned.1.call-start
  6.6 0.9 copy-done
  7.5 8.1 %multiply_reduce_fusion = (f32[32,8,4]{2,1,0:T(8,128)S(1)}, f32[32,8,4,512]{3,2,1,0:T(4,128)S(1)}) fusion(bf16[32,8,4,64]{3,2,1,0:T(4,128)(2,1)S(1)} %bitcast.14, bf16[32,512,8,64]{1,3,2,0:T(8,128)(2,1)} %param.4), kind=kOutput, calls=%fused_computation.3 | convolution fusion | flops 68156416 | bytes 19009536 | tf_op jit(solution)/shard_map/bgsd,bugd->bgsu/dot_general | solution.py:8
  15.6 1.1 fusion.1
  16.7 8.3 %fusion.3 = f32[32,8,4,64]{3,2,1,0:T(4,128)S(1)} fusion(bf16[32,512,8,64]{1,3,2,0:T(8,128)(2,1)} %param.5, f32[32,8,4,512]{3,2,1,0:T(4,128)S(1)} %get-tuple-element.11, f32[32,8,4]{2,1,0:T(8,128)S(1)} %get-tuple-element.10), kind=kOutput, calls=%fused_computation.6 | convolution fusion | flops 68681728 | bytes 19140608 | tf_op jit(solution)/shard_map/bgsu,bugd->bgsd/dot_general | solution.py:8
  25.0 1.7 %copy.51 = f32[32,8,4,1]{3,2,1,0:T(4,128)S(1)} copy(f32[32,8,4,1]{2,1,0,3:T(8,128)S(1)} %bitcast.18) | data formatting | bytes 8192 | tf_op jit(solution)/shard_map/broadcast_in_dim | solution.py:17
  26.7 1.7 %copy.52 = f32[32,8,4,1]{3,2,1,0:T(4,128)S(1)} copy(f32[32,8,4,1]{2,1,0,3:T(8,128)S(1)} %bitcast.17) | data formatting | bytes 8192 | tf_op jit(solution)/shard_map/broadcast_in_dim | solution.py:14
  28.4 0.6 pad_maximum_fusion
  29.0 0.9 copy.53
  29.9 0.1 all-gather.3.cloned.1.call-update
  29.9 57.7 %all-gather.3.cloned.1.call-done = f32[512,8,4,66]{3,1,2,0:T(8,128)} async-done(((f32[32,8,4,66]{3,1,2,0:T(8,128)}), f32[512,8,4,66]{3,1,2,0:T(8,128)}) %all-gather.3.cloned.1.call-update) | async-done | bytes 4325392 | tf_op jit(solution)/shard_map/all_gather | solution.py:28
  87.6 11.5 %fusion.10 = (f32[16,32,8,4,1]{4,2,3,1,0:T(8,128)}, f32[32,8,4]{1,2,0:T(4,128)S(1)}, f32[16,32,8,4,1]{4,2,3,1,0:T(8,128)}) fusion(f32[16,32,8,4,66]{4,2,3,1,0:T(8,128)} %bitcast.15), kind=kLoop, calls=%fused_computation.17 | loop fusion | flops 15360 | bytes 266240 | tf_op jit(solution)/shard_map/slice | solution.py:21
  99.1 6.3 %copy.65 = f32[16,32,8,4,1]{1,2,4,3,0:T(8,128)S(1)} copy(f32[16,32,8,4,1]{4,2,3,1,0:T(8,128)} %get-tuple-element.5) | data formatting | bytes 131072
  105.5 0.1 copy.66
  105.6 0.0 copy-start.1
  105.6 6.4 %copy.64 = f32[16,32,8,4,1]{1,2,4,3,0:T(8,128)S(1)} copy(f32[16,32,8,4,1]{4,2,3,1,0:T(8,128)} %get-tuple-element.7) | data formatting | bytes 131072
  112.0 0.1 multiply_reduce_fusion.1
  112.0 0.4 copy.55
  112.5 5.3 %fusion = f32[32,8,4,64]{3,1,2,0:T(8,128)S(1)} fusion(f32[16,32,8,4,66]{4,2,3,1,0:T(8,128)} %bitcast.16, f32[16,32,8,4]{2,3,1,0:T(4,128)S(1)} %copy.55), kind=kLoop, calls=%fused_computation.1 | loop fusion | flops 2031616 | bytes 4521984 | tf_op jit(solution)/shard_map/reduce_sum | solution.py:23
  117.7 0.3 copy.56
  118.0 0.2 fusion.7
  118.2 0.8 copy.59
  119.1 0.0 copy-done.1
  (1 shorter events, 0.0 us)
Async XLA Ops:
  6.5 1.0 copy-start
  6.6 81.0 %all-gather.3.cloned.1.call-start = ((), (), s32[]{:S(2)}) async-start(), calls=%async_computation | async-start | bytes 8912896 | tf_op jit(solution)/shard_map/all_gather | solution.py:28
  105.6 13.5 %copy-start.1 = (bf16[32,32,64]{2,1,0:T(8,128)(2,1)S(1)}, bf16[32,32,64]{2,1,0:T(8,128)(2,1)}, u32[]{:S(2)}) copy-start(bf16[32,32,64]{2,1,0:T(8,128)(2,1)} %param.3) | copy-start | bytes 393220
Sparse Core Ops, SparseCore 0:
  30.0 57.5 all-gather.2
where the time goes:
time: 126 us
  waiting for transfers between devices  57.7 us (46%)
  local copies, waits for them, and re-layouts  19.5 us (15%)
  other arithmetic  18.7 us (15%)
  matrix products  16.5 us (13%)
  between operations  13.5 us (11%)
    all_gather x1, waiting for transfers between devices, step(): return together(lax.all_gather(part_of(q, k, v), 'sp')).reshape(q.shape)  57.7 us
    dot_general x2, matrix products, einsum(): return jnp.einsum(form, a.astype(jnp.float32), b.astype(jnp.float32))  16.5 us
    unnamed x7, local copies, waits for them, and re-layouts  13.8 us
    slice x1, other arithmetic, together(): seen, total, high = (parts[..., :-2], parts[..., -2:-1], parts[..., -1:])  11.5 us
    reduce_sum x1, other arithmetic, together(): jnp.sum(seen * scale, 0) / jnp.sum(total * scale, 0)  5.25 us
  transfers between devices with their start and end apart: 1, of which 1 were waited for; matrix products, arithmetic and copies ran while one was open for 0% of the time, Pallas kernels for 0%

commit v1 on v0

v1 whole, which is shorter than its diff:
```python
import functools

import jax
import jax.numpy as jnp
from jax import lax
from jax.experimental import pallas as pl
from jax.experimental.pallas import tpu as pltpu
from jax.sharding import PartitionSpec as P

LOG2E = 1.4426950408889634
GROUP = 4
AHEAD = 8
MESH = pl.DeviceIdType.MESH


def iota(shape, dim):
    return lax.broadcasted_iota(jnp.int32, shape, dim)


def spread(q, rows, width):
    d = q.shape[1]
    wide = jnp.concatenate([q] * (width // d), axis=1)
    mine = iota(wide.shape, 0) % rows // (rows * d // width) == iota(wide.shape, 1) // d
    return jnp.where(mine, wide, jnp.zeros_like(wide))


def fold(halves, d):
    ys = []
    for o in halves:
        rows, width = o.shape
        mine = iota(o.shape, 0) // (rows * d // width) == iota(o.shape, 1) // d
        x = jnp.where(mine, o, 0.0)
        y = x[:, : 2 * d]
        for i in range(2 * d, width, 2 * d):
            y = y + x[:, i : i + 2 * d]
        ys.append(y + pltpu.roll(y, d, 1))
    return jnp.where(iota(ys[0].shape, 1) < d, ys[0], ys[1])


def as_row(columns, lanes):
    total = jnp.zeros((8, lanes), jnp.float32)
    at = iota(total.shape, 1) - iota(total.shape, 0)
    for i, column in enumerate(columns):
        for k in range(0, column.shape[0], 8):
            total = jnp.where(at == i * column.shape[0] + k, column[k : k + 8], total)
    return jnp.sum(total, axis=0, keepdims=True)


def kernel(n, q_ref, k_hbm, v_hbm, o_ref, kbuf, vbuf, pbuf, part, stat, got, gots, done, ksem, vsem, s_part, r_part, s_stat, r_stat, s_done, r_done):
    b = k_hbm.shape[0]
    d = q_ref.shape[2]
    rows = q_ref.shape[1] // 2
    lanes = 2 * d
    width = kbuf.shape[1] // 2
    me, dp = lax.axis_index("sp"), lax.axis_index("dp")
    others = sorted(range(1, n), key=lambda k: -min(k, n - k))
    to = {k: lax.rem(me + k, n) for k in others}
    frm = {k: lax.rem(me + n - k, n) for k in others}

    def keys(i):
        return pltpu.make_async_copy(k_hbm.at[i], kbuf.at[i], ksem.at[i])

    def values(i):
        return pltpu.make_async_copy(v_hbm.at[i], vbuf.at[i], vsem.at[i])

    for i in range(AHEAD):
        keys(i).start()
        values(i).start()
    barrier = pltpu.get_barrier_semaphore()
    for k in others:
        pl.semaphore_signal(barrier, inc=1, device_id=(dp, to[k]), device_id_type=MESH)

    def score(base):
        out = []
        for j in range(GROUP):
            q = spread(q_ref[base + j], rows, width)
            for h in range(2):
                out.append(jnp.dot(q[h * rows : (h + 1) * rows], kbuf[base + j, h * width : (h + 1) * width], preferred_element_type=jnp.float32))
        return out

    def soften(base, scores):
        for j in range(GROUP):
            ms, ls = [], []
            for h in range(2):
                s = scores[2 * j + h]
                m = jnp.max(s, axis=1, keepdims=True)
                p = jnp.exp2((s - m) * (d**-0.5 * LOG2E))
                pbuf[j, h * rows : (h + 1) * rows] = p.astype(jnp.bfloat16)
                ms.append(m * d**-0.5)
                ls.append(jnp.sum(p, axis=1, keepdims=True))
            stat[base + j] = as_row(ms + ls, lanes)

    def see(base):
        for j in range(GROUP):
            halves = [
                lax.dot_general(
                    pbuf[j, h * rows : (h + 1) * rows],
                    vbuf[base + j, h * width : (h + 1) * width],
                    (((1,), (1,)), ((), ())),
                    preferred_element_type=jnp.float32,
                )
                for h in range(2)
            ]
            part[base + j] = fold(halves, d).astype(jnp.bfloat16)

    def step(t, carry):
        base = t * GROUP
        for j in range(GROUP):
            i = base + j + AHEAD - GROUP

            @pl.when(i < b)
            def _():
                keys(i).start()
                values(i).start()

        for j in range(GROUP):
            keys(base + j).wait()
            values(base - GROUP + j).wait()
        scores = score(base)
        see(base - GROUP)
        soften(base, scores)
        return carry

    def part_copies(c, k, sender):
        src, dst = (me, to[k]) if sender else (frm[k], me)
        s = c * n + to[k]
        dev = dict(device_id=(dp, to[k]), device_id_type=MESH)
        return (
            pltpu.make_async_remote_copy(src_ref=part.at[s], dst_ref=got.at[c, src], send_sem=s_part.at[c, k], recv_sem=r_part.at[c, k], **dev),
            pltpu.make_async_remote_copy(src_ref=stat.at[s], dst_ref=gots.at[c, src], send_sem=s_stat.at[c, k], recv_sem=r_stat.at[c, k], **dev),
        )

    def done_copy(c, k, sender):
        src = me if sender else frm[k]
        return pltpu.make_async_remote_copy(
            src_ref=done.at[c * n + me],
            dst_ref=done.at[c * n + src],
            send_sem=s_done.at[c, k],
            recv_sem=r_done.at[c, k],
            device_id=(dp, to[k]),
            device_id_type=MESH,
        )

    def send_parts(c):
        for k in others:
            for copy in part_copies(c, k, True):
                copy.start()
        mine = c * n + me
        got[c, me] = part[mine]
        gots[c, me] = stat[mine]

    def put_together(c):
        for k in others:
            for copy in part_copies(c, k, False):
                copy.wait_recv()
        s = jnp.concatenate([gots[c, i] for i in range(n)], axis=0)
        e = jnp.exp(s - jnp.max(s, axis=0, keepdims=True))
        total = jnp.sum(e * pltpu.roll(s, lanes - 2 * rows, 1), axis=0, keepdims=True)
        f = e / total
        accs = []
        for k in range(0, rows, 8):
            at = iota((8, lanes), 1) // d * rows + k + iota((8, lanes), 0)
            acc = jnp.zeros((8, lanes), jnp.float32)
            for i in range(n):
                scale = jnp.take_along_axis(jnp.broadcast_to(f[i : i + 1], (8, lanes)), at, axis=1)
                acc += scale * got[c, i].astype(jnp.float32)[k : k + 8]
            accs.append(acc)
        done[c * n + me] = jnp.concatenate(accs, axis=0).astype(jnp.bfloat16)
        for k in others:
            done_copy(c, k, True).start()

    def lay_out(c):
        for k in others:
            done_copy(c, k, False).wait_recv()
        for i in range(n):
            x = done[c * n + i]
            o_ref[c * n + i, :rows] = x[:, :d]
            o_ref[c * n + i, rows:] = x[:, d:]

    for j in range(GROUP):
        keys(j).wait()
    soften(0, score(0))
    steps, chunks = b // GROUP, b // n
    t = 1
    for c in range(chunks - 1):
        upto = (c + 1) * n // GROUP + 1
        lax.fori_loop(t, upto, step, 0)
        t = upto
        if c == 0:
            pl.semaphore_wait(barrier, n - 1)
        send_parts(c)
    lax.fori_loop(t, steps, step, 0)
    for c in range(chunks - 1):
        put_together(c)
    for j in range(GROUP):
        values(b - GROUP + j).wait()
    see(b - GROUP)
    send_parts(chunks - 1)
    put_together(chunks - 1)
    for c in range(chunks):
        lay_out(c)
    for c in range(chunks):
        for k in others:
            for copy in part_copies(c, k, True):
                copy.wait_send()
            done_copy(c, k, True).wait_send()


def solution(mesh):
    n = mesh.shape["sp"]

    def step(q, k, v):
        b, u, g, d = k.shape
        heads = q.shape[1]
        rows, lanes = heads // 2, 2 * d
        k = jnp.transpose(k, (0, 2, 3, 1)).reshape(b, g * d, u)
        v = jnp.transpose(v, (0, 2, 3, 1)).reshape(b, g * d, u)
        c = b // n
        dma = pltpu.SemaphoreType.DMA
        return pl.pallas_call(
            functools.partial(kernel, n),
            out_shape=jax.ShapeDtypeStruct(q.shape, q.dtype),
            in_specs=[
                pl.BlockSpec(memory_space=pltpu.VMEM),
                pl.BlockSpec(memory_space=pl.ANY),
                pl.BlockSpec(memory_space=pl.ANY),
            ],
            out_specs=pl.BlockSpec(memory_space=pltpu.VMEM),
            scratch_shapes=[
                pltpu.VMEM((b, g * d, u), jnp.bfloat16),
                pltpu.VMEM((b, g * d, u), jnp.bfloat16),
                pltpu.VMEM((GROUP, heads, u), jnp.bfloat16),
                pltpu.VMEM((b, rows, lanes), jnp.bfloat16),
                pltpu.VMEM((b, 1, lanes), jnp.float32),
                pltpu.VMEM((c, n, rows, lanes), jnp.bfloat16),
                pltpu.VMEM((c, n, 1, lanes), jnp.float32),
                pltpu.VMEM((b, rows, lanes), jnp.bfloat16),
                dma((b,)),
                dma((b,)),
                dma((c, n)),
                dma((c, n)),
                dma((c, n)),
                dma((c, n)),
                dma((c, n)),
                dma((c, n)),
            ],
            compiler_params=pltpu.CompilerParams(collective_id=0, has_side_effects=True, vmem_limit_bytes=60 * 2**20),
        )(q, k, v)

    return jax.shard_map(
        step,
        mesh=mesh,
        in_specs=(P("dp", None, None), P("dp", "sp", None, None), P("dp", "sp", None, None)),
        out_specs=P("dp", None, None),
        check_vma=False,
    )
```

time: 126 us -> 38.1 us (0.30)
  waiting for transfers between devices: 57.7 us -> 0 us
  Pallas kernels: 0 us -> 36.3 us
  other arithmetic: 18.7 us -> 0 us
  local copies, waits for them, and re-layouts: 19.5 us -> 1.67 us
  matrix products: 16.5 us -> 0 us
  between operations: 13.5 us -> 0.01 us
    all_gather x1 -> x0, waiting for transfers between devices: 57.7 us -> none  [step(): return together(lax.all_gather(part_of(q, k, v), 'sp')).reshape(q.shape)]
    pallas_call x0 -> x1, Pallas kernels: none -> 36.3 us  [step(): pl.pallas_call(functools.partial(kernel, n), out_shape=jax.ShapeDtypeStru...]
    dot_general x2 -> x0, matrix products: 16.5 us -> none  [einsum(): return jnp.einsum(form, a.astype(jnp.float32), b.astype(jnp.float32))]
    unnamed x7 -> x1, local copies, waits for them, and re-layouts: 13.8 us -> 1.67 us
    slice x1 -> x0, other arithmetic: 11.5 us -> none  [together(): seen, total, high = (parts[..., :-2], parts[..., -2:-1], parts[..., -1:])]
    reduce_sum x3 -> x0, other arithmetic: 6.39 us -> none  [the longest x1 5.25 us: together(): jnp.sum(seen * scale, 0) / jnp.sum(total * scale, 0)]
    broadcast_in_dim x2 -> x0, local copies, waits for them, and re-layouts: 3.33 us -> none  [the longest x1 1.66 us: part_of(): jnp.sum(weights, -1, keepdims=True)]
  transfers between devices with their start and end apart: 1 -> 0, of which waited for: 1 -> 0; matrix products, arithmetic and copies ran while one was open for 0% -> 0% of each run, Pallas kernels for 0% -> 0%
where the time goes in v1:
time: 38.1 us; the launch traced here: 37.9 us
  Pallas kernels  36.3 us (95%)
  local copies, waits for them, and re-layouts  1.67 us (4%)
    pallas_call x1, Pallas kernels, step(): pl.pallas_call(functools.partial(kernel, n), out_shape=jax.ShapeDtypeStru...  36.3 us
    unnamed x1, local copies, waits for them, and re-layouts  1.67 us

profile of v1, /device:TPU:21, one launch (start us, length us, event | category | flops | bytes accessed | tf_op | source)
XLA Modules:
  0.0 37.9 jit_solution(172821144523219984)
XLA Ops:
  0.0 36.3 %shard_map.37 = bf16[32,32,64]{2,1,0:T(8,128)(2,1)} custom-call(bf16[32,32,64]{2,1,0:T(8,128)(2,1)} %q_ref.1, bf16[32,512,512]{2,1,0:T(8,128)(2,1)} %bitcast.6, bf16[32,512,512]{2,1,0:T(8,128)(2,1)} %bitcast.7), custom_call_target="tpu_custom_call" | custom-call | tf_op jit(solution)/shard_map/pallas_call | solution.py:220
  36.3 1.7 %copy.5 = bf16[32,32,64]{2,1,0:T(8,128)(2,1)} copy(bf16[32,32,64]{2,1,0:T(8,128)(2,1)} %shard_map.37) | data formatting | bytes 262144

commit v2 on v1

v2 whole, which is shorter than its diff:
```python
import functools

import jax
import jax.numpy as jnp
from jax import lax
from jax.experimental import pallas as pl
from jax.experimental.pallas import tpu as pltpu
from jax.sharding import PartitionSpec as P

LOG2E = 1.4426950408889634
GROUP = 4
AHEAD = 2
MESH = pl.DeviceIdType.MESH


def iota(shape, dim):
    return lax.broadcasted_iota(jnp.int32, shape, dim)


def spread(q, rows, width):
    d = q.shape[1]
    wide = jnp.concatenate([q] * (width // d), axis=1)
    mine = iota(wide.shape, 0) % rows // (rows * d // width) == iota(wide.shape, 1) // d
    return jnp.where(mine, wide, jnp.zeros_like(wide))


def fold(halves, d):
    ys = []
    for o in halves:
        rows, width = o.shape
        mine = iota(o.shape, 0) // (rows * d // width) == iota(o.shape, 1) // d
        x = jnp.where(mine, o, 0.0)
        y = x[:, : 2 * d]
        for i in range(2 * d, width, 2 * d):
            y = y + x[:, i : i + 2 * d]
        ys.append(y + pltpu.roll(y, d, 1))
    return jnp.where(iota(ys[0].shape, 1) < d, ys[0], ys[1])


def as_row(columns, lanes):
    total = jnp.zeros((8, lanes), jnp.float32)
    at = iota(total.shape, 1) - iota(total.shape, 0)
    for i, column in enumerate(columns):
        for k in range(0, column.shape[0], 8):
            total = jnp.where(at == i * column.shape[0] + k, column[k : k + 8], total)
    return jnp.sum(total, axis=0, keepdims=True)


def kernel(n, q_hbm, k_hbm, v_hbm, done, q_ref, kbuf, vbuf, pbuf, part, stat, got, gots, qsem, ksem, vsem, s_part, r_part, s_stat, r_stat, s_done, r_done):
    b = k_hbm.shape[0]
    steps, chunks = b // GROUP, b // n
    d = q_ref.shape[2]
    rows = q_ref.shape[1] // 2
    lanes = 2 * d
    width = kbuf.shape[1] // 2
    me, dp = lax.axis_index("sp"), lax.axis_index("dp")
    others = sorted(range(1, n), key=lambda k: -min(k, n - k))
    to = {k: jnp.where(me + k < n, me + k, me + k - n) for k in others}

    def keys(t):
        at = pl.ds(t * GROUP, GROUP)
        return pltpu.make_async_copy(k_hbm.at[at], kbuf.at[at], ksem.at[t])

    def values(t):
        at = pl.ds(t * GROUP, GROUP)
        return pltpu.make_async_copy(v_hbm.at[at], vbuf.at[at], vsem.at[t])

    queries = pltpu.make_async_copy(q_hbm, q_ref, qsem)
    queries.start()
    keys(0).start()
    barrier = pltpu.get_barrier_semaphore()
    for k in others:
        pl.semaphore_signal(barrier, inc=1, device_id=(dp, to[k]), device_id_type=MESH)

    for t in range(AHEAD):
        keys(t + 1).start()
        values(t).start()

    def score(base):
        out = []
        for j in range(GROUP):
            q = spread(q_ref[base + j], rows, width)
            for h in range(2):
                out.append(jnp.dot(q[h * rows : (h + 1) * rows], kbuf[base + j, h * width : (h + 1) * width], preferred_element_type=jnp.float32))
        return out

    def soften(base, scores):
        for j in range(GROUP):
            ms, ls = [], []
            for h in range(2):
                s = scores[2 * j + h]
                m = jnp.max(s, axis=1, keepdims=True)
                p = jnp.exp2((s - m) * (d**-0.5 * LOG2E))
                pbuf[j, h * rows : (h + 1) * rows] = p.astype(jnp.bfloat16)
                ms.append(m * d**-0.5)
                ls.append(jnp.sum(p, axis=1, keepdims=True))
            stat[base + j] = as_row(ms + ls, lanes)

    def see(base):
        for j in range(GROUP):
            halves = [
                lax.dot_general(
                    pbuf[j, h * rows : (h + 1) * rows],
                    vbuf[base + j, h * width : (h + 1) * width],
                    (((1,), (1,)), ((), ())),
                    preferred_element_type=jnp.float32,
                )
                for h in range(2)
            ]
            part[base + j] = fold(halves, d).astype(jnp.bfloat16)

    def step(t, carry):
        base = t * GROUP

        @pl.when(t + AHEAD < steps)
        def _():
            keys(t + AHEAD).start()

        @pl.when(t - 1 + AHEAD < steps)
        def _():
            values(t - 1 + AHEAD).start()

        @pl.when(t == 2)
        def _():
            pl.semaphore_wait(barrier, n - 1)

        @pl.when(t >= 2)
        def _():
            send_parts(t - 2)

        keys(t).wait()
        values(t - 1).wait()
        scores = score(base)
        see(base - GROUP)
        soften(base, scores)
        return carry

    def owner(s):
        return s % GROUP * (n // GROUP) + s // GROUP % (n // GROUP)

    def owned(c):
        return c * n + me % (n // GROUP) * GROUP + me // (n // GROUP)

    def sending(src, dst, send_sem, recv_sem, dev):
        return pltpu.make_async_remote_copy(src_ref=src, dst_ref=dst, send_sem=send_sem, recv_sem=recv_sem, device_id=(dp, dev), device_id_type=MESH)

    def send_parts(t):
        for j in range(GROUP):
            s = t * GROUP + j
            c, dev = s // n, owner(s)

            @pl.when(dev != me)
            def _():
                sending(part.at[s], got.at[c, me], s_part, r_part.at[c], dev).start()
                sending(stat.at[s], gots.at[c, me], s_stat, r_stat.at[c], dev).start()

    def put_together(c):
        with jax.named_scope("parts"):
            some = pl.ds(0, n - 1)
            sending(got.at[c, some], got.at[c, some], s_part, r_part.at[c], me).wait_recv()
            sending(gots.at[c, some], gots.at[c, some], s_stat, r_stat.at[c], me).wait_recv()
        mine = owned(c)
        got[c, me] = part[mine]
        gots[c, me] = stat[mine]
        s = jnp.concatenate([gots[c, i] for i in range(n)], axis=0)
        e = jnp.exp(s - jnp.max(s, axis=0, keepdims=True))
        total = jnp.sum(e * pltpu.roll(s, lanes - 2 * rows, 1), axis=0, keepdims=True)
        f = e / total
        accs = []
        for k in range(0, rows, 8):
            at = iota((8, lanes), 1) // d * rows + k + iota((8, lanes), 0)
            acc = jnp.zeros((8, lanes), jnp.float32)
            for i in range(n):
                scale = jnp.take_along_axis(jnp.broadcast_to(f[i : i + 1], (8, lanes)), at, axis=1)
                acc += scale * got[c, i].astype(jnp.float32)[k : k + 8]
            accs.append(acc)
        done[mine] = jnp.concatenate(accs, axis=0).astype(jnp.bfloat16)
        for k in others:
            sending(done.at[mine], done.at[mine], s_done, r_done, to[k]).start()

    S = jax.named_scope
    with S("first"):
        queries.wait()
        keys(0).wait()
        soften(0, score(0))
    with S("loop"):
        lax.fori_loop(1, steps, step, 0)
    with S("send"):
        send_parts(steps - 2)
    with S("last"):
        values(steps - 1).wait()
        see(b - GROUP)
    with S("send"):
        send_parts(steps - 1)
    for c in range(chunks):
        put_together(c)
    with S("gather"):
        some = pl.ds(0, chunks * (n - 1))
        sending(done.at[some], done.at[some], s_done, r_done, me).wait_recv()
    with S("drain"):
        sending(done.at[some], done.at[some], s_done, r_done, me).wait_send()
        sending(part.at[some], part.at[some], s_part, r_part.at[0], me).wait_send()
        sending(stat.at[some], stat.at[some], s_stat, r_stat.at[0], me).wait_send()


def lay_out(x_ref, o_ref):
    rows, d = x_ref.shape[1], o_ref.shape[2]
    for i in range(x_ref.shape[0]):
        x = x_ref[i]
        o_ref[i, :rows] = x[:, :d]
        o_ref[i, rows:] = x[:, d:]


def solution(mesh):
    n = mesh.shape["sp"]

    def step(q, k, v):
        b, u, g, d = k.shape
        heads = q.shape[1]
        rows, lanes = heads // 2, 2 * d
        k = jnp.transpose(k, (0, 2, 3, 1)).reshape(b, g * d, u)
        v = jnp.transpose(v, (0, 2, 3, 1)).reshape(b, g * d, u)
        c = b // n
        dma = pltpu.SemaphoreType.DMA
        done = pl.pallas_call(
            functools.partial(kernel, n),
            out_shape=pltpu.VMEM((b, rows, lanes), q.dtype),
            in_specs=[
                pl.BlockSpec(memory_space=pltpu.HBM),
                pl.BlockSpec(memory_space=pltpu.HBM),
                pl.BlockSpec(memory_space=pltpu.HBM),
            ],
            out_specs=pl.BlockSpec(memory_space=pltpu.VMEM),
            scratch_shapes=[
                pltpu.VMEM(q.shape, q.dtype),
                pltpu.VMEM((b, g * d, u), jnp.bfloat16),
                pltpu.VMEM((b, g * d, u), jnp.bfloat16),
                pltpu.VMEM((GROUP, heads, u), jnp.bfloat16),
                pltpu.VMEM((b, rows, lanes), jnp.bfloat16),
                pltpu.VMEM((b, 1, lanes), jnp.float32),
                pltpu.VMEM((c, n, rows, lanes), jnp.bfloat16),
                pltpu.VMEM((c, n, 1, lanes), jnp.float32),
                dma,
                dma((b // GROUP,)),
                dma((b // GROUP,)),
                dma,
                dma((c,)),
                dma,
                dma((c,)),
                dma,
                dma,
            ],
            compiler_params=pltpu.CompilerParams(collective_id=0, has_side_effects=True, vmem_limit_bytes=60 * 2**20),
        )(q, k, v)
        return pl.pallas_call(
            lay_out,
            out_shape=jax.ShapeDtypeStruct(q.shape, q.dtype),
            in_specs=[pl.BlockSpec(memory_space=pltpu.VMEM)],
            out_specs=pl.BlockSpec(memory_space=pltpu.VMEM),
            compiler_params=pltpu.CompilerParams(vmem_limit_bytes=8 * 2**20),
        )(done)

    return jax.shard_map(
        step,
        mesh=mesh,
        in_specs=(P("dp", None, None), P("dp", "sp", None, None), P("dp", "sp", None, None)),
        out_specs=P("dp", None, None),
        check_vma=False,
    )
```

time: 38.1 us -> 28.4 us (0.75)
  Pallas kernels: 36.3 us -> 28.3 us
  local copies, waits for them, and re-layouts: 1.67 us -> 0 us
    pallas_call x1 -> x2, Pallas kernels: 36.3 us -> 28.3 us  [the longest x1 27.4 us: step(): pl.pallas_call(functools.partial(kernel, n), out_shape=pltpu.VMEM((b, row...]
    unnamed x1 -> x0, local copies, waits for them, and re-layouts: 1.67 us -> none
where the time goes in v2:
time: 28.4 us; the launch traced here: 28.3 us
  Pallas kernels  28.3 us (100%)
    pallas_call x1, Pallas kernels, step(): pl.pallas_call(functools.partial(kernel, n), out_shape=pltpu.VMEM((b, row...  27.4 us
    pallas_call x1, Pallas kernels, step(): pl.pallas_call(lay_out, out_shape=jax.ShapeDtypeStruct(q.shape, q.dtype),...  0.85 us

profile of v2, /device:TPU:21, one launch (start us, length us, event | category | flops | bytes accessed | tf_op | source)
XLA Modules:
  0.0 28.3 jit_solution(2254458381200343769)
XLA Ops:
  0.0 27.4 %shard_map.37.x_ref = bf16[32,16,128]{2,1,0:T(8,128)(2,1)S(1)} custom-call(bf16[32,32,64]{2,1,0:T(8,128)(2,1)} %q_hbm.1, bf16[32,512,512]{2,1,0:T(8,128)(2,1)} %bitcast.6, bf16[32,512,512]{2,1,0:T(8,128)(2,1)} %bitcast.7), custom_call_target="tpu_custom_call" | custom-call | tf_op jit(solution)/shard_map/pallas_call | solution.py:225
  27.4 0.8 %shard_map.38 = bf16[32,32,64]{2,1,0:T(8,128)(2,1)} custom-call(bf16[32,16,128]{2,1,0:T(8,128)(2,1)S(1)} %shard_map.37.x_ref), custom_call_target="tpu_custom_call" | custom-call | tf_op jit(solution)/shard_map/pallas_call | solution.py:255

commit v3 on v2

--- a/solution.py
+++ b/solution.py
@@ -9,6 +9,7 @@
 
 LOG2E = 1.4426950408889634
 GROUP = 4
+HUBS = 2
 AHEAD = 2
 MESH = pl.DeviceIdType.MESH
 
@@ -135,11 +136,13 @@
         soften(base, scores)
         return carry
 
-    def owner(s):
-        return s % GROUP * (n // GROUP) + s // GROUP % (n // GROUP)
-
-    def owned(c):
-        return c * n + me % (n // GROUP) * GROUP + me // (n // GROUP)
+    early = n // GROUP
+
+    def owner(t, j):
+        first = jnp.where(t < steps - 2, n // 4, 0)
+        late = jnp.where(t == steps - 1, j % HUBS, first + j)
+        slot = jnp.where(t == steps - 1, steps - 1 - early + 1 + j // HUBS, t - early + 1)
+        return jnp.where(t < early, j * early + t, late), jnp.where(t < early, 0, slot)
 
     def sending(src, dst, send_sem, recv_sem, dev):
         return pltpu.make_async_remote_copy(src_ref=src, dst_ref=dst, send_sem=send_sem, recv_sem=recv_sem, device_id=(dp, dev), device_id_type=MESH)
@@ -147,22 +150,21 @@
     def send_parts(t):
         for j in range(GROUP):
             s = t * GROUP + j
-            c, dev = s // n, owner(s)
+            dev, slot = owner(t, j)
 
             @pl.when(dev != me)
             def _():
-                sending(part.at[s], got.at[c, me], s_part, r_part.at[c], dev).start()
-                sending(stat.at[s], gots.at[c, me], s_stat, r_stat.at[c], dev).start()
-
-    def put_together(c):
+                sending(part.at[s], got.at[slot, me], s_part, r_part.at[slot], dev).start()
+                sending(stat.at[s], gots.at[slot, me], s_stat, r_stat.at[slot], dev).start()
+
+    def put_together(slot, mine):
         with jax.named_scope("parts"):
             some = pl.ds(0, n - 1)
-            sending(got.at[c, some], got.at[c, some], s_part, r_part.at[c], me).wait_recv()
-            sending(gots.at[c, some], gots.at[c, some], s_stat, r_stat.at[c], me).wait_recv()
-        mine = owned(c)
-        got[c, me] = part[mine]
-        gots[c, me] = stat[mine]
-        s = jnp.concatenate([gots[c, i] for i in range(n)], axis=0)
+            sending(got.at[slot, some], got.at[slot, some], s_part, r_part.at[slot], me).wait_recv()
+            sending(gots.at[slot, some], gots.at[slot, some], s_stat, r_stat.at[slot], me).wait_recv()
+        got[slot, me] = part[mine]
+        gots[slot, me] = stat[mine]
+        s = jnp.concatenate([gots[slot, i] for i in range(n)], axis=0)
         e = jnp.exp(s - jnp.max(s, axis=0, keepdims=True))
         total = jnp.sum(e * pltpu.roll(s, lanes - 2 * rows, 1), axis=0, keepdims=True)
         f = e / total
@@ -172,11 +174,14 @@
             acc = jnp.zeros((8, lanes), jnp.float32)
             for i in range(n):
                 scale = jnp.take_along_axis(jnp.broadcast_to(f[i : i + 1], (8, lanes)), at, axis=1)
-                acc += scale * got[c, i].astype(jnp.float32)[k : k + 8]
+                acc += scale * got[slot, i].astype(jnp.float32)[k : k + 8]
             accs.append(acc)
         done[mine] = jnp.concatenate(accs, axis=0).astype(jnp.bfloat16)
-        for k in others:
-            sending(done.at[mine], done.at[mine], s_done, r_done, to[k]).start()
+        for dev in range(n):
+
+            @pl.when(dev != me)
+            def _():
+                sending(done.at[mine], done.at[mine], s_done, r_done, dev).start()
 
     S = jax.named_scope
     with S("first"):
@@ -192,15 +197,46 @@
         see(b - GROUP)
     with S("send"):
         send_parts(steps - 1)
-    for c in range(chunks):
-        put_together(c)
-    with S("gather"):
-        some = pl.ds(0, chunks * (n - 1))
-        sending(done.at[some], done.at[some], s_done, r_done, me).wait_recv()
-    with S("drain"):
-        sending(done.at[some], done.at[some], s_done, r_done, me).wait_send()
-        sending(part.at[some], part.at[some], s_part, r_part.at[0], me).wait_send()
-        sending(stat.at[some], stat.at[some], s_stat, r_stat.at[0], me).wait_send()
+    put_together(0, me % early * GROUP + me // early)
+    own = jnp.int32(1)
+    for t in range(early, steps):
+        for j in range(GROUP):
+            if t < steps - 1 and j:
+                continue
+            if t < steps - 1:
+                dev, slot = owner(t, 0)
+                at = me - dev
+                mine = (at >= 0) & (at < GROUP)
+            else:
+                dev, slot = owner(t, j)
+                at, mine = j, dev == me
+                if j % HUBS:
+                    continue
+                at = j + me
+                mine = me < HUBS
+            own = own + mine.astype(jnp.int32)
+            slot = t - early + 1 if t < steps - 1 else steps - early + j // HUBS
+
+            @pl.when(mine)
+            def _():
+                put_together(slot, t * GROUP + at)
+
+    pool = got.reshape(got.shape[0] * n, rows, lanes)
+    pools = gots.reshape(gots.shape[0] * n, 1, lanes)
+
+    def pooled(count):
+        return pool.at[pl.ds(0, count)]
+
+    for c in range(1, 2 + GROUP):
+
+        @pl.when(own == c)
+        def _():
+            with jax.named_scope("gather"):
+                sending(pooled(b - c), pooled(b - c), s_done, r_done, me).wait_recv()
+            with jax.named_scope("drain"):
+                sending(pooled((n - 1) * c), pooled(b - c), s_done, r_done, me).wait_send()
+                sending(pooled(b - c), pooled(b - c), s_part, r_part.at[0], me).wait_send()
+                sending(pools.at[pl.ds(0, b - c)], pools.at[pl.ds(0, b - c)], s_stat, r_stat.at[0], me).wait_send()
 
 
 def lay_out(x_ref, o_ref):
@@ -220,7 +256,7 @@
         rows, lanes = heads // 2, 2 * d
         k = jnp.transpose(k, (0, 2, 3, 1)).reshape(b, g * d, u)
         v = jnp.transpose(v, (0, 2, 3, 1)).reshape(b, g * d, u)
-        c = b // n
+        c = b // GROUP - n // GROUP + GROUP // HUBS
         dma = pltpu.SemaphoreType.DMA
         done = pl.pallas_call(
             functools.partial(kernel, n),

time: 28.4 us -> 26.8 us (0.944)
  Pallas kernels: 28.3 us -> 26.7 us
    pallas_call x1, Pallas kernels: 27.4 us -> 25.9 us  [step(): pl.pallas_call(functools.partial(kernel, n), out_shape=pltpu.VMEM((b, row...]
where the time goes in v3:
time: 26.8 us; the launch traced here: 26.7 us
  Pallas kernels  26.7 us (100%)
    pallas_call x1, Pallas kernels, step(): pl.pallas_call(functools.partial(kernel, n), out_shape=pltpu.VMEM((b, row...  25.9 us
    pallas_call x1, Pallas kernels, step(): pl.pallas_call(lay_out, out_shape=jax.ShapeDtypeStruct(q.shape, q.dtype),...  0.85 us

profile of v3, /device:TPU:21, one launch (start us, length us, event | category | flops | bytes accessed | tf_op | source)
XLA Modules:
  0.0 26.7 jit_solution(95298087289883170)
XLA Ops:
  0.0 25.9 %shard_map.37.x_ref = bf16[32,16,128]{2,1,0:T(8,128)(2,1)S(1)} custom-call(bf16[32,32,64]{2,1,0:T(8,128)(2,1)} %q_hbm.1, bf16[32,512,512]{2,1,0:T(8,128)(2,1)} %bitcast.6, bf16[32,512,512]{2,1,0:T(8,128)(2,1)} %bitcast.7), custom_call_target="tpu_custom_call" | custom-call | tf_op jit(solution)/shard_map/pallas_call | solution.py:261
  25.9 0.8 %shard_map.38 = bf16[32,32,64]{2,1,0:T(8,128)(2,1)} custom-call(bf16[32,16,128]{2,1,0:T(8,128)(2,1)S(1)} %shard_map.37.x_ref), custom_call_target="tpu_custom_call" | custom-call | tf_op jit(solution)/shard_map/pallas_call | solution.py:291

commit v4 on v3

--- a/solution.py
+++ b/solution.py
@@ -10,6 +10,7 @@
 LOG2E = 1.4426950408889634
 GROUP = 4
 HUBS = 2
+SLOTS = 4
 AHEAD = 2
 MESH = pl.DeviceIdType.MESH
 
@@ -47,7 +48,7 @@
     return jnp.sum(total, axis=0, keepdims=True)
 
 
-def kernel(n, q_hbm, k_hbm, v_hbm, done, q_ref, kbuf, vbuf, pbuf, part, stat, got, gots, qsem, ksem, vsem, s_part, r_part, s_stat, r_stat, s_done, r_done):
+def kernel(n, q_hbm, k_hbm, v_hbm, done, q_ref, kbuf, vbuf, pbuf, part, stat, got, gots, qsem, ksem, vsem, s_part, r_part, s_done, r_done):
     b = k_hbm.shape[0]
     steps, chunks = b // GROUP, b // n
     d = q_ref.shape[2]
@@ -60,11 +61,11 @@
 
     def keys(t):
         at = pl.ds(t * GROUP, GROUP)
-        return pltpu.make_async_copy(k_hbm.at[at], kbuf.at[at], ksem.at[t])
+        return pltpu.make_async_copy(k_hbm.at[at], kbuf.at[at], ksem.at[t % SLOTS])
 
     def values(t):
         at = pl.ds(t * GROUP, GROUP)
-        return pltpu.make_async_copy(v_hbm.at[at], vbuf.at[at], vsem.at[t])
+        return pltpu.make_async_copy(v_hbm.at[at], vbuf.at[at], vsem.at[t % SLOTS])
 
     queries = pltpu.make_async_copy(q_hbm, q_ref, qsem)
     queries.start()
@@ -136,10 +137,11 @@
         soften(base, scores)
         return carry
 
+    pools = gots.reshape(gots.shape[0] * n, 1, lanes)
     early = n // GROUP
 
     def owner(t, j):
-        first = jnp.where(t < steps - 2, n // 4, 0)
+        first = jnp.where(t < steps - 2, n // 4, n - GROUP)
         late = jnp.where(t == steps - 1, j % HUBS, first + j)
         slot = jnp.where(t == steps - 1, steps - 1 - early + 1 + j // HUBS, t - early + 1)
         return jnp.where(t < early, j * early + t, late), jnp.where(t < early, 0, slot)
@@ -155,13 +157,12 @@
             @pl.when(dev != me)
             def _():
                 sending(part.at[s], got.at[slot, me], s_part, r_part.at[slot], dev).start()
-                sending(stat.at[s], gots.at[slot, me], s_stat, r_stat.at[slot], dev).start()
+                sending(stat.at[s], gots.at[slot, me], s_part, r_part.at[slot], dev).start()
 
     def put_together(slot, mine):
         with jax.named_scope("parts"):
-            some = pl.ds(0, n - 1)
-            sending(got.at[slot, some], got.at[slot, some], s_part, r_part.at[slot], me).wait_recv()
-            sending(gots.at[slot, some], gots.at[slot, some], s_stat, r_stat.at[slot], me).wait_recv()
+            rest = pools.at[pl.ds(0, (n - 1) * (rows // 2 + 1))]
+            sending(rest, rest, s_part, r_part.at[slot], me).wait_recv()
         got[slot, me] = part[mine]
         gots[slot, me] = stat[mine]
         s = jnp.concatenate([gots[slot, i] for i in range(n)], axis=0)
@@ -222,7 +223,6 @@
                 put_together(slot, t * GROUP + at)
 
     pool = got.reshape(got.shape[0] * n, rows, lanes)
-    pools = gots.reshape(gots.shape[0] * n, 1, lanes)
 
     def pooled(count):
         return pool.at[pl.ds(0, count)]
@@ -235,8 +235,8 @@
                 sending(pooled(b - c), pooled(b - c), s_done, r_done, me).wait_recv()
             with jax.named_scope("drain"):
                 sending(pooled((n - 1) * c), pooled(b - c), s_done, r_done, me).wait_send()
-                sending(pooled(b - c), pooled(b - c), s_part, r_part.at[0], me).wait_send()
-                sending(pools.at[pl.ds(0, b - c)], pools.at[pl.ds(0, b - c)], s_stat, r_stat.at[0], me).wait_send()
+                rest = pools.at[pl.ds(0, (b - c) * (rows // 2 + 1))]
+                sending(rest, rest, s_part, r_part.at[0], me).wait_send()
 
 
 def lay_out(x_ref, o_ref):
@@ -275,12 +275,10 @@
                 pltpu.VMEM((b, rows, lanes), jnp.bfloat16),
                 pltpu.VMEM((b, 1, lanes), jnp.float32),
                 pltpu.VMEM((c, n, rows, lanes), jnp.bfloat16),
-                pltpu.VMEM((c, n, 1, lanes), jnp.float32),
+                pltpu.VMEM((-(-b * (rows // 2 + 1) // n), n, 1, lanes), jnp.float32),
                 dma,
-                dma((b // GROUP,)),
-                dma((b // GROUP,)),
-                dma,
-                dma((c,)),
+                dma((SLOTS,)),
+                dma((SLOTS,)),
                 dma,
                 dma((c,)),
                 dma,

time: 26.8 us -> 26.5 us (0.989)
  Pallas kernels: 26.7 us -> 26.4 us
    pallas_call x1, Pallas kernels: 25.9 us -> 25.6 us  [step(): pl.pallas_call(functools.partial(kernel, n), out_shape=pltpu.VMEM((b, row...]
where the time goes in v4:
time: 26.5 us; the launch traced here: 26.4 us
  Pallas kernels  26.4 us (100%)
    pallas_call x1, Pallas kernels, step(): pl.pallas_call(functools.partial(kernel, n), out_shape=pltpu.VMEM((b, row...  25.6 us
    pallas_call x1, Pallas kernels, step(): pl.pallas_call(lay_out, out_shape=jax.ShapeDtypeStruct(q.shape, q.dtype),...  0.85 us

profile of v4, /device:TPU:21, one launch (start us, length us, event | category | flops | bytes accessed | tf_op | source)
XLA Modules:
  0.0 26.4 jit_solution(3501466048779879733)
XLA Ops:
  0.0 25.6 %shard_map.37.x_ref = bf16[32,16,128]{2,1,0:T(8,128)(2,1)S(1)} custom-call(bf16[32,32,64]{2,1,0:T(8,128)(2,1)} %q_hbm.1, bf16[32,512,512]{2,1,0:T(8,128)(2,1)} %bitcast.6, bf16[32,512,512]{2,1,0:T(8,128)(2,1)} %bitcast.7), custom_call_target="tpu_custom_call" | custom-call | tf_op jit(solution)/shard_map/pallas_call | solution.py:261
  25.6 0.8 %shard_map.38 = bf16[32,32,64]{2,1,0:T(8,128)(2,1)} custom-call(bf16[32,16,128]{2,1,0:T(8,128)(2,1)S(1)} %shard_map.37.x_ref), custom_call_target="tpu_custom_call" | custom-call | tf_op jit(solution)/shard_map/pallas_call | solution.py:289

commit v5 on v4

--- a/solution.py
+++ b/solution.py
@@ -239,12 +239,20 @@
                 sending(rest, rest, s_part, r_part.at[0], me).wait_send()
 
 
-def lay_out(x_ref, o_ref):
+def lay_out(x_ref, o_hbm, o_ref, sem):
     rows, d = x_ref.shape[1], o_ref.shape[2]
-    for i in range(x_ref.shape[0]):
-        x = x_ref[i]
-        o_ref[i, :rows] = x[:, :d]
-        o_ref[i, rows:] = x[:, d:]
+    per = x_ref.shape[0] // 4
+    copies = []
+    for c in range(4):
+        for i in range(c * per, (c + 1) * per):
+            x = x_ref[i]
+            o_ref[i, :rows] = x[:, :d]
+            o_ref[i, rows:] = x[:, d:]
+        at = pl.ds(c * per, per)
+        copies.append(pltpu.make_async_copy(o_ref.at[at], o_hbm.at[at], sem.at[c]))
+        copies[-1].start()
+    for copy in copies:
+        copy.wait()
 
 
 def solution(mesh):
@@ -290,7 +298,8 @@
             lay_out,
             out_shape=jax.ShapeDtypeStruct(q.shape, q.dtype),
             in_specs=[pl.BlockSpec(memory_space=pltpu.VMEM)],
-            out_specs=pl.BlockSpec(memory_space=pltpu.VMEM),
+            out_specs=pl.BlockSpec(memory_space=pltpu.HBM),
+            scratch_shapes=[pltpu.VMEM(q.shape, q.dtype), pltpu.SemaphoreType.DMA((4,))],
             compiler_params=pltpu.CompilerParams(vmem_limit_bytes=8 * 2**20),
         )(done)
 

time: 26.5 us -> 26.5 us (level)
  no operation moved by 1% of the time
where the time goes in v5:
time: 26.5 us; the launch traced here: 26.4 us
  Pallas kernels  26.4 us (100%)
    pallas_call x1, Pallas kernels, step(): pl.pallas_call(functools.partial(kernel, n), out_shape=pltpu.VMEM((b, row...  25.6 us
    pallas_call x1, Pallas kernels, step(): pl.pallas_call(lay_out, out_shape=jax.ShapeDtypeStruct(q.shape, q.dtype),...  0.81 us

profile of v5, /device:TPU:21, one launch (start us, length us, event | category | flops | bytes accessed | tf_op | source)
XLA Modules:
  0.0 26.4 jit_solution(11772159553634527163)
XLA Ops:
  0.0 25.6 %shard_map.37.x_ref = bf16[32,16,128]{2,1,0:T(8,128)(2,1)S(1)} custom-call(bf16[32,32,64]{2,1,0:T(8,128)(2,1)} %q_hbm.1, bf16[32,512,512]{2,1,0:T(8,128)(2,1)} %bitcast.6, bf16[32,512,512]{2,1,0:T(8,128)(2,1)} %bitcast.7), custom_call_target="tpu_custom_call" | custom-call | tf_op jit(solution)/shard_map/pallas_call | solution.py:269
  25.6 0.8 %shard_map.38 = bf16[32,32,64]{2,1,0:T(8,128)(2,1)} custom-call(bf16[32,16,128]{2,1,0:T(8,128)(2,1)S(1)} %shard_map.37.x_ref), custom_call_target="tpu_custom_call" | custom-call | tf_op jit(solution)/shard_map/pallas_call | solution.py:297
